TPU v7x, 32 devices: a whole 2x2x4 slice. The times are simulated.
32 devices in a mesh: dp: 4 (over y, x), tensor: 8 (over z, core).
Axes of the slice: x: 2, y: 2, z: 4, core: 2. Of those that a mesh axis runs over, the one named last changes fastest.
Arguments:
- noisy: bfloat16 [32, 256, 1152], P('dp', None, 'tensor'), may hold values from -6 to 6
- labels: int32 [32], P('dp'), may hold values from 0 to 999
- tsteps: int32 [32], P('dp'), may hold values from 0 to 999
- guide_index: int32 [32], P('dp'), may hold values from 0 to 31
- class_table: bfloat16 [1001, 1152], replicated, may hold values from -6 to 6
- time_table: bfloat16 [1000, 1152], replicated, may hold values from -6 to 6
- guide_table: bfloat16 [32, 1152], replicated, may hold values from -6 to 6
- guide_weights: float32 [32], replicated, may hold values from 0.5 to 4
- teacher_qkv: bfloat16 [1152, 3456], P(None, 'tensor'), may hold values from -0.1875 to 0.1875
- teacher_out: bfloat16 [1152, 1152], P('tensor'), may hold values from -0.1875 to 0.1875
- teacher_ada: bfloat16 [3, 1152, 1152], P(None, None, 'tensor'), may hold values from -0.1875 to 0.1875
- student_qkv: bfloat16 [1152, 3456], P(None, 'tensor'), may hold values from -0.1875 to 0.1875
- student_out: bfloat16 [1152, 1152], P('tensor'), may hold values from -0.1875 to 0.1875
- student_ada: bfloat16 [3, 1152, 1152], P(None, None, 'tensor'), may hold values from -0.1875 to 0.1875
Outputs:
- grad_qkv: float32 [1152, 3456], P('dp', 'tensor')
- grad_out: float32 [1152, 1152], P('tensor', 'dp')
- grad_ada: float32 [3, 1152, 1152], P(None, 'dp', 'tensor')
All inputs are finite; a program needn't handle non-finite values.
Results may differ from a plain program's by a relative error of at most 0.034.
Values may be sent and summed in bfloat16 or wider, within the bound.
A program may use at most 128 MiB of HBM per device.

v0:
```python
import math
import jax
import jax.numpy as jnp
from jax import lax
from jax.sharding import PartitionSpec as P

HD = 72
norm_eps = 1e-06


def lookup_rows(indices, table_rows):
    one_hot = (
        indices[:, None] == jnp.arange(table_rows.shape[0], dtype=jnp.int32)[None, :]
    ).astype(table_rows.dtype)
    return jnp.dot(one_hot, table_rows, preferred_element_type=jnp.float32)


def attend(qkv_sums, heads_here):
    batch_rows, seq_len = (qkv_sums.shape[0], qkv_sums.shape[1])
    heads_qkv = qkv_sums.astype(jnp.bfloat16).reshape(batch_rows, seq_len, heads_here, 3, HD)
    queries, key_rows, values = (
        heads_qkv[:, :, :, 0],
        heads_qkv[:, :, :, 1],
        heads_qkv[:, :, :, 2],
    )
    scores = jnp.einsum(
        "blhe,bmhe->bhlm", queries, key_rows, preferred_element_type=jnp.float32
    ) * (1.0 / math.sqrt(HD))
    exponent = jnp.exp(scores - jnp.max(scores, axis=-1, keepdims=True))
    attn_prob = exponent / jnp.sum(exponent, axis=-1, keepdims=True)
    prob_low = attn_prob.astype(jnp.bfloat16)
    attn_mixed = jnp.einsum("bhlm,bmhe->blhe", prob_low, values, preferred_element_type=jnp.float32)
    attn_mixed = attn_mixed.astype(jnp.bfloat16).reshape(batch_rows, seq_len, heads_here * HD)
    return (heads_qkv, attn_prob, prob_low, attn_mixed)


def attend_grad(heads_qkv, attn_prob, prob_low, grad_low):
    batch_rows, seq_len = (heads_qkv.shape[0], heads_qkv.shape[1])
    queries, key_rows, values = (
        heads_qkv[:, :, :, 0],
        heads_qkv[:, :, :, 1],
        heads_qkv[:, :, :, 2],
    )
    grad_probs = jnp.einsum("blhe,bmhe->bhlm", grad_low, values, preferred_element_type=jnp.float32)
    row_delta = jnp.sum(attn_prob * grad_probs, axis=-1, keepdims=True)
    grad_scores = (attn_prob * (grad_probs - row_delta) * (1.0 / math.sqrt(HD))).astype(
        jnp.bfloat16
    )
    grad_query = jnp.einsum(
        "bhlm,bmhe->blhe", grad_scores, key_rows, preferred_element_type=jnp.float32
    )
    grad_keys = jnp.einsum(
        "bhlm,blhe->bmhe", grad_scores, queries, preferred_element_type=jnp.float32
    )
    grad_values = jnp.einsum(
        "bhlm,blhe->bmhe", prob_low, grad_low, preferred_element_type=jnp.float32
    )
    grad_qkv_act = jnp.stack([grad_query, grad_keys, grad_values], axis=3).astype(jnp.bfloat16)
    return grad_qkv_act.reshape(batch_rows, seq_len, -1)


def forward(source, embed_act, qkv_weight, out_weight, ada_weight):
    heads_here = out_weight.shape[0] // HD
    modulation = jnp.einsum(
        "bd,kde->bke", embed_act, ada_weight, preferred_element_type=jnp.float32
    )
    wide_mod = lax.all_gather(modulation, "tensor", axis=2, tiled=True)
    full_rows = (
        source.astype(jnp.float32) * (1.0 + wide_mod[:, 1][:, None]) + wide_mod[:, 0][:, None]
    ).astype(jnp.bfloat16)
    qkv_sums = jnp.einsum("bld,df->blf", full_rows, qkv_weight, preferred_element_type=jnp.float32)
    heads_qkv, attn_prob, prob_low, attn_mixed = attend(qkv_sums, heads_here)
    partial_value = jnp.einsum(
        "blf,fd->bld", attn_mixed, out_weight, preferred_element_type=jnp.float32
    )
    projected = lax.psum_scatter(
        partial_value.astype(jnp.bfloat16), "tensor", scatter_dimension=2, tiled=True
    ).astype(jnp.float32)
    branch = modulation[:, 2][:, None] * projected
    return (branch, (full_rows, heads_qkv, attn_prob, prob_low, attn_mixed, projected, modulation))


def local(
    noisy,
    labels,
    tsteps,
    guide_index,
    class_table,
    time_table,
    guide_table,
    guide_weights,
    teacher_qkv,
    teacher_out,
    teacher_ada,
    student_qkv,
    student_out,
    student_ada,
):
    samples, seq_len, width_part = noisy.shape
    model_width = width_part * lax.axis_size("tensor")
    batch_size = samples * lax.axis_size("dp")
    signal = noisy.astype(jnp.float32)
    row_sums = lax.psum((jnp.sum(signal, axis=2), jnp.sum(signal * signal, axis=2)), "tensor")
    row_mean = row_sums[0] / model_width
    row_var = row_sums[1] / model_width - row_mean * row_mean
    normed = ((signal - row_mean[:, :, None]) * lax.rsqrt(row_var + norm_eps)[:, :, None]).astype(
        jnp.bfloat16
    )
    null_class = class_table.shape[0] - 1
    time_embed = lookup_rows(tsteps, time_table)
    cond_embed = lookup_rows(labels, class_table) + time_embed
    null_embed = class_table[null_class].astype(jnp.float32)[None, :] + time_embed
    guide_hot = guide_index[:, None] == jnp.arange(guide_table.shape[0], dtype=jnp.int32)[None, :]
    student_embed = cond_embed + jnp.dot(
        guide_hot.astype(jnp.bfloat16), guide_table, preferred_element_type=jnp.float32
    )
    strength = jnp.sum(jnp.where(guide_hot, guide_weights[None, :], 0.0), axis=1)
    cond_act = jax.nn.silu(cond_embed).astype(jnp.bfloat16)
    null_act = jax.nn.silu(null_embed).astype(jnp.bfloat16)
    student_act = jax.nn.silu(student_embed).astype(jnp.bfloat16)
    scale_norm = 1.0 / math.sqrt(batch_size * seq_len)
    wide_rows = lax.all_gather(normed, "tensor", axis=2, tiled=True)
    teacher_full = jnp.concatenate([wide_rows, wide_rows], axis=0)
    teacher_act = jnp.concatenate([cond_act, null_act], axis=0)
    teacher_branch, unused_saved = forward(
        teacher_full, teacher_act, teacher_qkv, teacher_out, teacher_ada
    )
    teacher_update = teacher_branch.astype(jnp.bfloat16).astype(jnp.float32)
    scaled = strength[:, None, None]
    target = signal + (
        (1.0 + scaled) * teacher_update[:samples] - scaled * teacher_update[samples:]
    )
    branch, saved = forward(wide_rows, student_act, student_qkv, student_out, student_ada)
    full_rows, heads_qkv, attn_prob, prob_low, attn_mixed, projected, modulation = saved
    heads_here = student_out.shape[0] // HD
    cotangent = (signal + branch - target) * scale_norm
    grad_gate = jnp.sum(cotangent * projected, axis=1)
    grad_proj = (cotangent * modulation[:, 2][:, None]).astype(jnp.bfloat16)
    gathered = lax.all_gather(grad_proj, "tensor", axis=2, tiled=True)
    grad_mixed = jnp.einsum(
        "bld,ed->ble", gathered, student_out, preferred_element_type=jnp.float32
    )
    block_grad = jnp.einsum("ble,bld->ed", attn_mixed, gathered, preferred_element_type=jnp.float32)
    grad_mixed, grad_out_rows = (grad_mixed, block_grad)
    grad_low = grad_mixed.astype(jnp.bfloat16).reshape(samples, seq_len, heads_here, HD)
    grad_qkv_act = attend_grad(heads_qkv, attn_prob, prob_low, grad_low)
    grad_qkv_local = jnp.einsum(
        "bld,blf->df", full_rows, grad_qkv_act, preferred_element_type=jnp.float32
    )
    input_terms = jnp.einsum(
        "blf,df->bld", grad_qkv_act, student_qkv, preferred_element_type=jnp.float32
    )
    grad_input = lax.psum_scatter(
        input_terms.astype(jnp.bfloat16), "tensor", scatter_dimension=2, tiled=True
    ).astype(jnp.float32)
    grad_shift = jnp.sum(grad_input, axis=1)
    grad_scale = jnp.sum(grad_input * normed.astype(jnp.float32), axis=1)
    grad_modulation = jnp.stack([grad_shift, grad_scale, grad_gate], axis=1)
    grad_ada_local = jnp.einsum(
        "bd,bke->kde",
        student_act.astype(jnp.float32),
        grad_modulation,
        precision=lax.Precision.HIGHEST,
    )
    grad_qkv, grad_out, grad_ada = (
        lax.psum_scatter(
            grad_qkv_local.astype(jnp.bfloat16), "dp", scatter_dimension=0, tiled=True
        ).astype(jnp.float32),
        lax.psum_scatter(
            grad_out_rows.astype(jnp.bfloat16), "dp", scatter_dimension=1, tiled=True
        ).astype(jnp.float32),
        lax.psum_scatter(
            grad_ada_local.astype(jnp.bfloat16), "dp", scatter_dimension=1, tiled=True
        ).astype(jnp.float32),
    )
    return (grad_qkv, grad_out, grad_ada)


def solution(mesh):
    return jax.shard_map(
        local,
        mesh=mesh,
        in_specs=(
            P("dp", None, "tensor"),
            P("dp"),
            P("dp"),
            P("dp"),
            P(),
            P(),
            P(),
            P(),
            P(None, "tensor"),
            P("tensor", None),
            P(None, None, "tensor"),
            P(None, "tensor"),
            P("tensor", None),
            P(None, None, "tensor"),
        ),
        out_specs=(P("dp", "tensor"), P("tensor", "dp"), P(None, "dp", "tensor")),
        check_vma=False,
    )
```

profile of v0, /device:TPU:0, one launch (start us, length us, event | category | flops | bytes accessed | tf_op | source)
XLA Modules:
  0.0 544.9 jit_solution(2838430340158237559)
XLA Ops:
  8.6 30.3 %all-reduce = (f32[8,256]{1,0:T(8,128)S(1)}, f32[8,256]{1,0:T(8,128)S(1)}) all-reduce(f32[8,256]{1,0:T(8,128)S(1)} %get-tuple-element.6, f32[8,256]{1,0:T(8,128)S(1)} %get-tuple-element.5), channel_id=1, replica_groups=mesh['dp'=4,'tensor'=8] {'tensor'}, use_global_device_ids=true, to_apply=%region_3.0 | all-reduce | flops 4096 | bytes 32768 | tf_op jit(solution)/shard_map/psum | solution.py:103
  45.7 40.4 %all_gather.14 = f32[16,3,1152]{0,1,2:T(4,128)S(1)} all-gather(f32[16,3,144]{0,1,2:T(4,128)S(1)} %copy.72), channel_id=1, replica_groups=mesh['dp'=4,'tensor'=8] {'tensor'}, dimensions={2}, use_global_device_ids=true | all-gather | bytes 248832 | tf_op jit(solution)/shard_map/all_gather | solution.py:67
  87.4 18.4 %all-gather.3.cloned.1.call-done = bf16[8,256,1152]{1,2,0:T(8,128)(2,1)} async-done(((bf16[8,256,144]{1,2,0:T(8,128)(2,1)}), bf16[8,256,1152]{1,2,0:T(8,128)(2,1)}) %all-gather.3.cloned.1.call-update) | async-done | bytes 4718608 | tf_op jit(solution)/shard_map/all_gather | solution.py:122
  105.8 10.8 %fusion.31 = bf16[16,256,432]{1,2,0:T(8,128)(2,1)S(1)} fusion(bf16[8,256,1152]{1,2,0:T(8,128)(2,1)} %all-gather.3.cloned.1.call-done, f32[16,1152]{1,0:T(8,128)S(1)} %copy.74, f32[16,1152]{1,0:T(8,128)S(1)} %copy.73, bf16[1152,432]{0,1:T(8,128)(2,1)} %param.22), kind=kOutput, calls=%fused_computation.35 | convolution fusion | flops 4111663104 | bytes 9400320 | tf_op jit(solution)/shard_map/bld,df->blf/dot_general | solution.py:71
  119.7 6.3 %fusion.94 = (f32[16,2,256]{2,1,0:T(2,128)S(1)}, f32[16,2,256,256]{2,3,1,0:T(8,128)S(1)}) fusion(f32[16,2,256,256]{2,3,1,0:T(8,128)S(1)} %fusion.59), kind=kOutput, calls=%fused_computation.132 | output fusion | flops 8388863 | bytes 16809984 | tf_op jit(solution)/shard_map/sub | solution.py:29
  128.3 5.3 convolution_convert_fusion
  135.5 42.4 %all_gather.13 = f32[8,3,1152]{0,1,2:T(4,128)S(1)} all-gather(f32[8,3,144]{0,1,2:T(4,128)S(1)} %copy.64), channel_id=1, replica_groups=mesh['dp'=4,'tensor'=8] {'tensor'}, dimensions={2}, use_global_device_ids=true | all-gather | bytes 124416 | tf_op jit(solution)/shard_map/all_gather | solution.py:67
  179.3 5.9 %fusion.36 = bf16[8,256,432]{1,2,0:T(8,128)(2,1)S(1)} fusion(bf16[8,256,1152]{1,2,0:T(8,128)(2,1)} %all-gather.3.cloned.1.call-done, f32[8,1152]{1,0:T(8,128)S(1)} %copy.66, f32[8,1152]{1,0:T(8,128)S(1)} %copy.65, bf16[1152,432]{0,1:T(8,128)(2,1)S(1)} %copy-done.13), kind=kOutput, calls=%fused_computation.50 | convolution fusion | flops 2048753664 | bytes 7557120 | tf_op jit(solution)/shard_map/bld,df->blf/dot_general | solution.py:71
  191.2 3.6 convolution_convert_fusion.2
  195.1 54.8 %reduce-scatter.13.cloned.1.call-done = bf16[16,256,144]{1,2,0:T(8,128)(2,1)} async-done(((bf16[16,256,1152]{1,2,0:T(8,128)(2,1)}), bf16[16,256,144]{1,2,0:T(8,128)(2,1)}) %reduce-scatter.13.cloned.1.call-update) | async-done | bytes 1179664 | tf_op jit(solution)/shard_map/reduce_scatter | solution.py:76
  253.0 54.6 %reduce-scatter.11.cloned.1.call-done = bf16[8,256,144]{1,2,0:T(8,128)(2,1)} async-done(((bf16[8,256,1152]{1,2,0:T(8,128)(2,1)}), bf16[8,256,144]{1,2,0:T(8,128)(2,1)}) %reduce-scatter.11.cloned.1.call-update) | async-done | bytes 589840 | tf_op jit(solution)/shard_map/reduce_scatter | solution.py:76
  311.6 49.6 %all-gather.5.cloned.1.call-done = bf16[8,256,1152]{1,2,0:T(8,128)(2,1)} async-done(((bf16[8,256,144]{1,2,0:T(8,128)(2,1)}), bf16[8,256,1152]{1,2,0:T(8,128)(2,1)}) %all-gather.5.cloned.1.call-update) | async-done | bytes 4718608 | tf_op jit(solution)/shard_map/all_gather | solution.py:139
  361.2 3.4 convolution_convert_fusion.4
  365.6 3.8 fusion.66
  369.4 7.7 %fusion.48 = bf16[8,256,2,1,72]{1,4,2,0,3:T(8,128)(2,1)S(1)} fusion(f32[8,2,256,256]{2,3,1,0:T(8,128)} %fusion.66, bf16[8,256,2,3,72]{1,4,3,2,0:T(8,128)(2,1)} %bitcast.136, f32[8,2,256,256]{2,3,1,0:T(8,128)} %copy-done.3, f32[8,2,256]{2,1,0:T(2,128)S(1)} %get-tuple-element.17), kind=kOutput, calls=%fused_computation.63 | convolution fusion | flops 158634240 | bytes 17989632 | tf_op jit(solution)/shard_map/bhlm,bmhe->blhe/dot_general | solution.py:49
  377.1 7.6 %fusion.45 = bf16[8,256,2,1,72]{1,4,2,0,3:T(8,128)(2,1)S(1)} fusion(f32[8,2,256,256]{2,3,1,0:T(8,128)} %fusion.66, bf16[8,256,2,3,72]{1,4,3,2,0:T(8,128)(2,1)} %bitcast.137, f32[8,2,256,256]{2,3,1,0:T(8,128)} %copy-done.3, f32[8,2,256]{2,1,0:T(2,128)S(1)} %get-tuple-element.17), kind=kOutput, calls=%fused_computation.62 | convolution fusion | flops 158634240 | bytes 17989632 | tf_op jit(solution)/shard_map/bhlm,blhe->bmhe/dot_general | solution.py:52
  386.3 4.4 convolution_convert_fusion.1
  390.8 4.0 fusion.32
  395.9 6.4 %fusion.23 = bf16[1152,432]{1,0:T(8,128)(2,1)} fusion(bf16[8,256,432]{1,2,0:T(8,128)(2,1)} %bitcast.132, bf16[8,256,1152]{1,2,0:T(8,128)(2,1)} %all-gather.3.cloned.1.call-done, f32[8,1152]{1,0:T(8,128)S(1)} %copy.66, f32[8,1152]{1,0:T(8,128)S(1)} %copy.65), kind=kOutput, calls=%fused_computation.29 | convolution fusion | flops 2048366592 | bytes 7557120 | tf_op jit(solution)/shard_map/bld,blf->df/dot_general | solution.py:147
  402.6 41.9 %reduce-scatter.17.cloned.1.call-done = bf16[8,256,144]{1,2,0:T(8,128)(2,1)} async-done(((bf16[8,256,1152]{1,2,0:T(8,128)(2,1)}), bf16[8,256,144]{1,2,0:T(8,128)(2,1)}) %reduce-scatter.17.cloned.1.call-update) | async-done | bytes 589840 | tf_op jit(solution)/shard_map/reduce_scatter | solution.py:153
  450.5 5.6 %reshape.56 = bf16[1152,432]{1,0:T(8,128)(2,1)} reshape(bf16[1152,3,144]{2,1,0:T(4,128)(2,1)} %bitcast.120) | data formatting | bytes 1990656
  456.0 15.7 %reduce-scatter.19.cloned.1.call-done = bf16[288,144]{1,0:T(8,128)(2,1)} async-done(((bf16[1152,144]{1,0:T(8,128)(2,1)}), bf16[288,144]{1,0:T(8,128)(2,1)}) %reduce-scatter.19.cloned.1.call-update) | async-done | bytes 82960
  473.5 29.9 %reduce-scatter.15.cloned.1.call-done = bf16[288,432]{1,0:T(8,128)(2,1)} async-done(((bf16[1152,432]{1,0:T(8,128)(2,1)}), bf16[288,432]{1,0:T(8,128)(2,1)}) %reduce-scatter.15.cloned.1.call-update) | async-done | bytes 248848 | tf_op jit(solution)/shard_map/reduce_scatter | solution.py:166
  505.2 29.8 %reduce-scatter.21.cloned.1.call-done = bf16[288,432]{1,0:T(8,128)(2,1)} async-done(((bf16[1152,432]{1,0:T(8,128)(2,1)}), bf16[288,432]{1,0:T(8,128)(2,1)}) %reduce-scatter.21.cloned.1.call-update) | async-done | bytes 248848
  (95 shorter events, 47.8 us)
Async XLA Ops:
  7.2 34.6 %copy-start = (bf16[1000,1152]{1,0:T(8,128)(2,1)S(1)}, bf16[1000,1152]{1,0:T(8,128)(2,1)}, u32[]{:S(2)}) copy-start(bf16[1000,1152]{1,0:T(8,128)(2,1)} %param.19) | copy-start | bytes 6912004
  7.2 35.7 %copy-start.12 = (s32[8]{0:T(128)S(1)}, s32[8]{0:T(128)}, u32[]{:S(2)}) copy-start(s32[8]{0:T(128)} %param.15) | copy-start | bytes 100
  7.2 37.9 %copy-start.9 = (bf16[3,1152,144]{1,2,0:T(8,128)(2,1)S(1)}, bf16[3,1152,144]{1,2,0:T(8,128)(2,1)}, u32[]{:S(2)}) copy-start(bf16[3,1152,144]{1,2,0:T(8,128)(2,1)} %param.24) | copy-start | bytes 2985988
  7.2 98.6 %all-gather.3.cloned.1.call-start = ((), (), s32[]{:S(2)}) async-start(), calls=%async_computation.6 | async-start | bytes 5308416 | tf_op jit(solution)/shard_map/all_gather | solution.py:122
  41.0 208.9 %reduce-scatter.13.cloned.1.call-start = ((), (), s32[]{:S(2)}) async-start(), calls=%async_computation.8 | async-start | bytes 10616832 | tf_op jit(solution)/shard_map/reduce_scatter | solution.py:76
  116.6 1.8 copy-start.7
  126.0 2.3 copy-start.11
  133.6 1.3 copy-start.10
  133.7 45.6 %copy-start.13 = (bf16[1152,432]{0,1:T(8,128)(2,1)S(1)}, bf16[1152,432]{0,1:T(8,128)(2,1)}, u32[]{:S(2)}) copy-start(bf16[1152,432]{0,1:T(8,128)(2,1)} %param.25) | copy-start | bytes 2985988
  133.7 173.9 %reduce-scatter.11.cloned.1.call-start = ((), (), s32[]{:S(2)}) async-start(), calls=%async_computation.7 | async-start | bytes 5308416 | tf_op jit(solution)/shard_map/reduce_scatter | solution.py:76
  185.2 4.0 copy-start.6
  189.2 2.0 copy-start.3
  189.2 2.0 copy-start.8
  191.2 3.7 copy-start.17
  194.8 112.8 %copy-start.2 = (bf16[8,256,144]{1,2,0:T(8,128)(2,1)S(1)}, bf16[8,256,144]{1,2,0:T(8,128)(2,1)}, u32[]{:S(2)}) copy-start(bf16[8,256,144]{1,2,0:T(8,128)(2,1)} %param.14) | copy-start | bytes 1769476
  194.9 166.3 %all-gather.5.cloned.1.call-start = ((), (), s32[]{:S(2)}) async-start(), calls=%async_computation.9 | async-start | bytes 5308416 | tf_op jit(solution)/shard_map/all_gather | solution.py:139
  311.3 133.2 %reduce-scatter.17.cloned.1.call-start = ((), (), s32[]{:S(2)}) async-start(), calls=%async_computation.11 | async-start | bytes 5308416 | tf_op jit(solution)/shard_map/reduce_scatter | solution.py:153
  361.2 3.6 copy-start.4
  384.7 1.5 copy-start.14
  385.1 1.2 copy-start.5
  390.7 81.0 %reduce-scatter.19.cloned.1.call-start = ((), (), s32[]{:S(2)}) async-start(), calls=%async_computation.12 | async-start | bytes 737280
  395.8 107.5 %reduce-scatter.15.cloned.1.call-start = ((), (), s32[]{:S(2)}) async-start(), calls=%async_computation.10 | async-start | bytes 1474560 | tf_op jit(solution)/shard_map/reduce_scatter | solution.py:166
  402.3 132.7 %reduce-scatter.21.cloned.1.call-start = ((), (), s32[]{:S(2)}) async-start(), calls=%async_computation.13 | async-start | bytes 1474560
  450.5 87.6 %copy-start.1 = (bf16[1000,1152]{1,0:T(8,128)(2,1)S(1)}, bf16[1000,1152]{1,0:T(8,128)(2,1)}, u32[]{:S(2)}) copy-start(bf16[1000,1152]{1,0:T(8,128)(2,1)} %param.19) | copy-start | bytes 6912004
  (2 other events, 1.8 us)
Sparse Core Ops, SparseCore 0:
  41.1 64.6 all-gather.2
  133.8 116.0 reduce-scatter.12
  252.2 55.3 reduce-scatter.10
  311.5 49.6 all-gather.4
  390.9 53.6 reduce-scatter.16
  447.8 23.8 reduce-scatter.18
  474.6 28.6 reduce-scatter.14
  506.3 28.6 reduce-scatter.20
where the time goes:
time: 546 us; the launch traced here: 545 us
  waiting for transfers between devices  295 us (54%)
  blocking collectives  113 us (21%)
  matrix products  73.9 us (14%)
  other arithmetic  27.9 us (5%)
  local copies, waits for them, and re-layouts  19.9 us (4%)
  between operations  14.5 us (3%)
    reduce_scatter x2, waiting for transfers between devices, forward(): lax.psum_scatter(partial_value.astype(jnp.bfloat16), 'tensor', scatter_di...  109 us
    all_gather x2, blocking collectives, forward(): wide_mod = lax.all_gather(modulation, 'tensor', axis=2, tiled=True)  82.8 us
    all_gather x1, waiting for transfers between devices, local(): gathered = lax.all_gather(grad_proj, 'tensor', axis=2, tiled=True)  49.6 us
    unnamed x10, waiting for transfers between devices  45.6 us
    reduce_scatter x1, waiting for transfers between devices, local(): lax.psum_scatter(input_terms.astype(jnp.bfloat16), 'tensor', scatter_dime...  41.9 us
    psum x1, blocking collectives, local(): lax.psum((jnp.sum(signal, axis=2), jnp.sum(signal * signal, axis=2)), 'te...  30.3 us
    reduce_scatter x1, waiting for transfers between devices, local(): lax.psum_scatter(grad_qkv_local.astype(jnp.bfloat16), 'dp', scatter_dimen...  29.9 us
    unnamed x42, local copies, waits for them, and re-layouts  18.7 us
  transfers between devices with their start and end apart: 8, of which 8 were waited for; matrix products, arithmetic and copies ran while one was open for 10% of the time, Pallas kernels for 0%

commit v1 on v0

--- a/solution.py
+++ b/solution.py
@@ -64,7 +64,14 @@
     modulation = jnp.einsum(
         "bd,kde->bke", embed_act, ada_weight, preferred_element_type=jnp.float32
     )
-    wide_mod = lax.all_gather(modulation, "tensor", axis=2, tiled=True)
+    ring = [modulation]
+    for hop in range(7):
+        ring.append(lax.ppermute(ring[-1], "tensor", [(dev, (dev + 1) % 8) for dev in range(8)]))
+    wide_mod = jnp.roll(
+        jnp.concatenate(ring[::-1], axis=2),
+        (lax.axis_index("tensor") + 1) * ring[0].shape[2],
+        axis=2,
+    )
     full_rows = (
         source.astype(jnp.float32) * (1.0 + wide_mod[:, 1][:, None]) + wide_mod[:, 0][:, None]
     ).astype(jnp.bfloat16)

time: 546 us -> 517 us (0.947)
  blocking collectives: 113 us -> 30.3 us
  waiting for transfers between devices: 295 us -> 349 us
    ppermute x0 -> x14, waiting for transfers between devices: none -> 83.4 us  [forward(): lax.ppermute(ring[-1], 'tensor', [(dev, (dev + 1) % 8) for dev in range(8)])]
    all_gather x2 -> x0, blocking collectives: 82.8 us -> none  [forward(): wide_mod = lax.all_gather(modulation, 'tensor', axis=2, tiled=True)]
    all_gather x1, waiting for transfers between devices: 18.4 us -> 3.35 us  [local(): wide_rows = lax.all_gather(normed, 'tensor', axis=2, tiled=True)]
    reduce_scatter x2, waiting for transfers between devices: 109 us -> 95.1 us  [forward(): lax.psum_scatter(partial_value.astype(jnp.bfloat16), 'tensor', scatter_di...]
  transfers between devices with their start and end apart: 8 -> 22, of which waited for: 8 -> 22; matrix products, arithmetic and copies ran while one was open for 10% -> 10% of each run, Pallas kernels for 0% -> 0%
where the time goes in v1:
time: 517 us; the launch traced here: 516 us
  waiting for transfers between devices  349 us (68%)
  matrix products  76 us (15%)
  blocking collectives  30.3 us (6%)
  other arithmetic  26.2 us (5%)
  local copies, waits for them, and re-layouts  19 us (4%)
  between operations  14.5 us (3%)
    reduce_scatter x2, waiting for transfers between devices, forward(): lax.psum_scatter(partial_value.astype(jnp.bfloat16), 'tensor', scatter_di...  95.1 us
    ppermute x14, waiting for transfers between devices, forward(): lax.ppermute(ring[-1], 'tensor', [(dev, (dev + 1) % 8) for dev in range(8)])  83.4 us
    all_gather x1, waiting for transfers between devices, local(): gathered = lax.all_gather(grad_proj, 'tensor', axis=2, tiled=True)  49.8 us
    unnamed x10, waiting for transfers between devices  45.7 us
    reduce_scatter x1, waiting for transfers between devices, local(): lax.psum_scatter(input_terms.astype(jnp.bfloat16), 'tensor', scatter_dime...  42 us
    psum x1, blocking collectives, local(): lax.psum((jnp.sum(signal, axis=2), jnp.sum(signal * signal, axis=2)), 'te...  30.3 us
    reduce_scatter x1, waiting for transfers between devices, local(): lax.psum_scatter(grad_qkv_local.astype(jnp.bfloat16), 'dp', scatter_dimen...  29.9 us
    unnamed x42, local copies, waits for them, and re-layouts  18.4 us
  transfers between devices with their start and end apart: 22, of which 22 were waited for; matrix products, arithmetic and copies ran while one was open for 10% of the time, Pallas kernels for 0%

profile of v1, /device:TPU:0, one launch (start us, length us, event | category | flops | bytes accessed | tf_op | source)
XLA Modules:
  0.0 516.2 jit_solution(6401181193630638002)
XLA Ops:
  8.6 30.3 %all-reduce = (f32[8,256]{1,0:T(8,128)S(1)}, f32[8,256]{1,0:T(8,128)S(1)}) all-reduce(f32[8,256]{1,0:T(8,128)S(1)} %get-tuple-element.6, f32[8,256]{1,0:T(8,128)S(1)} %get-tuple-element.5), channel_id=1, replica_groups=mesh['dp'=4,'tensor'=8] {'tensor'}, use_global_device_ids=true, to_apply=%region_3.0 | all-reduce | flops 4096 | bytes 32768 | tf_op jit(solution)/shard_map/psum | solution.py:110
  51.0 6.5 %collective-permute-done.8 = f32[16,3,144]{2,0,1:T(8,128)S(1)} collective-permute-done((f32[16,3,144]{2,0,1:T(8,128)S(1)}, f32[16,3,144]{2,0,1:T(8,128)S(1)}, u32[]{:S(2)}, u32[]{:S(2)}) %collective-permute-start.8) | collective-permute-done | bytes 27680 | tf_op jit(solution)/shard_map/ppermute | solution.py:69
  57.5 6.5 %collective-permute-done.9 = f32[16,3,144]{2,0,1:T(8,128)S(1)} collective-permute-done((f32[16,3,144]{2,0,1:T(8,128)S(1)}, f32[16,3,144]{2,0,1:T(8,128)S(1)}, u32[]{:S(2)}, u32[]{:S(2)}) %collective-permute-start.9) | collective-permute-done | bytes 27680 | tf_op jit(solution)/shard_map/ppermute | solution.py:69
  64.1 6.5 %collective-permute-done.10 = f32[16,3,144]{2,0,1:T(8,128)S(1)} collective-permute-done((f32[16,3,144]{2,0,1:T(8,128)S(1)}, f32[16,3,144]{2,0,1:T(8,128)S(1)}, u32[]{:S(2)}, u32[]{:S(2)}) %collective-permute-start.10) | collective-permute-done | bytes 27680 | tf_op jit(solution)/shard_map/ppermute | solution.py:69
  70.6 6.5 %collective-permute-done.11 = f32[16,3,144]{2,0,1:T(8,128)S(1)} collective-permute-done((f32[16,3,144]{2,0,1:T(8,128)S(1)}, f32[16,3,144]{2,0,1:T(8,128)S(1)}, u32[]{:S(2)}, u32[]{:S(2)}) %collective-permute-start.11) | collective-permute-done | bytes 27680 | tf_op jit(solution)/shard_map/ppermute | solution.py:69
  77.1 6.5 %collective-permute-done.12 = f32[16,3,144]{2,0,1:T(8,128)S(1)} collective-permute-done((f32[16,3,144]{2,0,1:T(8,128)S(1)}, f32[16,3,144]{2,0,1:T(8,128)S(1)}, u32[]{:S(2)}, u32[]{:S(2)}) %collective-permute-start.12) | collective-permute-done | bytes 27680 | tf_op jit(solution)/shard_map/ppermute | solution.py:69
  83.6 6.5 %collective-permute-done.13 = f32[16,3,144]{2,0,1:T(8,128)S(1)} collective-permute-done((f32[16,3,144]{2,0,1:T(8,128)S(1)}, f32[16,3,144]{2,0,1:T(8,128)S(1)}, u32[]{:S(2)}, u32[]{:S(2)}) %collective-permute-start.13) | collective-permute-done | bytes 27680 | tf_op jit(solution)/shard_map/ppermute | solution.py:69
  93.8 10.8 %fusion.31 = bf16[16,256,432]{1,2,0:T(8,128)(2,1)S(1)} fusion(bf16[8,256,1152]{1,2,0:T(8,128)(2,1)} %all-gather.3.cloned.1.call-done, f32[16,1152]{1,0:T(8,128)S(1)} %get-tuple-element.12, f32[16,1152]{1,0:T(8,128)S(1)} %get-tuple-element.11, bf16[1152,432]{0,1:T(8,128)(2,1)S(1)} %copy-done.12), kind=kOutput, calls=%fused_computation.35 | convolution fusion | flops 4111663104 | bytes 9400320 | tf_op jit(solution)/shard_map/bld,df->blf/dot_general | solution.py:78
  107.6 6.3 %fusion.96 = (f32[16,2,256]{2,1,0:T(2,128)S(1)}, f32[16,2,256,256]{2,3,1,0:T(8,128)S(1)}) fusion(f32[16,2,256,256]{2,3,1,0:T(8,128)S(1)} %fusion.59), kind=kOutput, calls=%fused_computation.136 | output fusion | flops 8388863 | bytes 16809984 | tf_op jit(solution)/shard_map/sub | solution.py:29
  128.3 5.7 %collective-permute-done.1 = f32[8,3,144]{2,0,1:T(8,128)S(1)} collective-permute-done((f32[8,3,144]{2,0,1:T(8,128)S(1)}, f32[8,3,144]{2,0,1:T(8,128)S(1)}, u32[]{:S(2)}, u32[]{:S(2)}) %collective-permute-start.1) | collective-permute-done | bytes 13856 | tf_op jit(solution)/shard_map/ppermute | solution.py:69
  139.7 5.7 %collective-permute-done.3 = f32[8,3,144]{2,0,1:T(8,128)S(1)} collective-permute-done((f32[8,3,144]{2,0,1:T(8,128)S(1)}, f32[8,3,144]{2,0,1:T(8,128)S(1)}, u32[]{:S(2)}, u32[]{:S(2)}) %collective-permute-start.3) | collective-permute-done | bytes 13856 | tf_op jit(solution)/shard_map/ppermute | solution.py:69
  151.1 5.7 %collective-permute-done.5 = f32[8,3,144]{2,0,1:T(8,128)S(1)} collective-permute-done((f32[8,3,144]{2,0,1:T(8,128)S(1)}, f32[8,3,144]{2,0,1:T(8,128)S(1)}, u32[]{:S(2)}, u32[]{:S(2)}) %collective-permute-start.5) | collective-permute-done | bytes 13856 | tf_op jit(solution)/shard_map/ppermute | solution.py:69
  156.8 5.7 %collective-permute-done.6 = f32[8,3,144]{2,0,1:T(8,128)S(1)} collective-permute-done((f32[8,3,144]{2,0,1:T(8,128)S(1)}, f32[8,3,144]{2,0,1:T(8,128)S(1)}, u32[]{:S(2)}, u32[]{:S(2)}) %collective-permute-start.6) | collective-permute-done | bytes 13856 | tf_op jit(solution)/shard_map/ppermute | solution.py:69
  162.8 5.9 %fusion.36 = bf16[8,256,432]{1,2,0:T(8,128)(2,1)S(1)} fusion(bf16[8,256,1152]{1,2,0:T(8,128)(2,1)} %all-gather.3.cloned.1.call-done, f32[8,1152]{1,0:T(8,128)S(1)} %get-tuple-element.14, f32[8,1152]{1,0:T(8,128)S(1)} %get-tuple-element.13, bf16[1152,432]{0,1:T(8,128)(2,1)S(1)} %copy-done.13), kind=kOutput, calls=%fused_computation.50 | convolution fusion | flops 2048753664 | bytes 7557120 | tf_op jit(solution)/shard_map/bld,df->blf/dot_general | solution.py:78
  178.8 42.8 %reduce-scatter.13.cloned.1.call-done = bf16[16,256,144]{1,2,0:T(8,128)(2,1)} async-done(((bf16[16,256,1152]{1,2,0:T(8,128)(2,1)}), bf16[16,256,144]{1,2,0:T(8,128)(2,1)}) %reduce-scatter.13.cloned.1.call-update) | async-done | bytes 1179664 | tf_op jit(solution)/shard_map/reduce_scatter | solution.py:83
  224.7 52.3 %reduce-scatter.11.cloned.1.call-done = bf16[8,256,144]{1,2,0:T(8,128)(2,1)} async-done(((bf16[8,256,1152]{1,2,0:T(8,128)(2,1)}), bf16[8,256,144]{1,2,0:T(8,128)(2,1)}) %reduce-scatter.11.cloned.1.call-update) | async-done | bytes 589840 | tf_op jit(solution)/shard_map/reduce_scatter | solution.py:83
  280.8 49.8 %all-gather.5.cloned.1.call-done = bf16[8,256,1152]{1,2,0:T(8,128)(2,1)} async-done(((bf16[8,256,144]{1,2,0:T(8,128)(2,1)}), bf16[8,256,1152]{1,2,0:T(8,128)(2,1)}) %all-gather.5.cloned.1.call-update) | async-done | bytes 4718608 | tf_op jit(solution)/shard_map/all_gather | solution.py:146
  337.7 7.6 %fusion.48 = bf16[8,256,2,1,72]{1,4,2,0,3:T(8,128)(2,1)S(1)} fusion(f32[8,2,256,256]{2,3,1,0:T(8,128)} %fusion.66, bf16[8,256,2,3,72]{1,4,3,2,0:T(8,128)(2,1)} %bitcast.136, f32[8,2,256,256]{2,3,1,0:T(8,128)} %copy-done.3, f32[8,2,256]{2,1,0:T(2,128)S(1)} %get-tuple-element.17), kind=kOutput, calls=%fused_computation.63 | convolution fusion | flops 158634240 | bytes 17989632 | tf_op jit(solution)/shard_map/bhlm,bmhe->blhe/dot_general | solution.py:49
  345.3 7.7 %fusion.45 = bf16[8,256,2,1,72]{1,4,2,0,3:T(8,128)(2,1)S(1)} fusion(f32[8,2,256,256]{2,3,1,0:T(8,128)} %fusion.66, bf16[8,256,2,3,72]{1,4,3,2,0:T(8,128)(2,1)} %bitcast.137, f32[8,2,256,256]{2,3,1,0:T(8,128)} %copy-done.3, f32[8,2,256]{2,1,0:T(2,128)S(1)} %get-tuple-element.17), kind=kOutput, calls=%fused_computation.62 | convolution fusion | flops 158634240 | bytes 17989632 | tf_op jit(solution)/shard_map/bhlm,blhe->bmhe/dot_general | solution.py:52
  367.1 6.4 %fusion.23 = bf16[1152,432]{1,0:T(8,128)(2,1)} fusion(bf16[8,256,432]{1,2,0:T(8,128)(2,1)} %bitcast.132, bf16[8,256,1152]{1,2,0:T(8,128)(2,1)} %all-gather.3.cloned.1.call-done, f32[8,1152]{1,0:T(8,128)S(1)} %get-tuple-element.14, f32[8,1152]{1,0:T(8,128)S(1)} %get-tuple-element.13), kind=kOutput, calls=%fused_computation.29 | convolution fusion | flops 2048366592 | bytes 7557120 | tf_op jit(solution)/shard_map/bld,blf->df/dot_general | solution.py:154
  373.8 42.0 %reduce-scatter.17.cloned.1.call-done = bf16[8,256,144]{1,2,0:T(8,128)(2,1)} async-done(((bf16[8,256,1152]{1,2,0:T(8,128)(2,1)}), bf16[8,256,144]{1,2,0:T(8,128)(2,1)}) %reduce-scatter.17.cloned.1.call-update) | async-done | bytes 589840 | tf_op jit(solution)/shard_map/reduce_scatter | solution.py:160
  427.2 15.7 %reduce-scatter.19.cloned.1.call-done = bf16[288,144]{1,0:T(8,128)(2,1)} async-done(((bf16[1152,144]{1,0:T(8,128)(2,1)}), bf16[288,144]{1,0:T(8,128)(2,1)}) %reduce-scatter.19.cloned.1.call-update) | async-done | bytes 82960
  444.7 29.9 %reduce-scatter.15.cloned.1.call-done = bf16[288,432]{1,0:T(8,128)(2,1)} async-done(((bf16[1152,432]{1,0:T(8,128)(2,1)}), bf16[288,432]{1,0:T(8,128)(2,1)}) %reduce-scatter.15.cloned.1.call-update) | async-done | bytes 248848 | tf_op jit(solution)/shard_map/reduce_scatter | solution.py:173
  476.5 29.8 %reduce-scatter.21.cloned.1.call-done = bf16[288,432]{1,0:T(8,128)(2,1)} async-done(((bf16[1152,432]{1,0:T(8,128)(2,1)}), bf16[288,432]{1,0:T(8,128)(2,1)}) %reduce-scatter.21.cloned.1.call-update) | async-done | bytes 248848
  (117 shorter events, 102.7 us)
Async XLA Ops:
  7.2 86.6 %all-gather.3.cloned.1.call-start = ((), (), s32[]{:S(2)}) async-start(), calls=%async_computation.6 | async-start | bytes 5308416 | tf_op jit(solution)/shard_map/all_gather | solution.py:129
  41.0 180.6 %reduce-scatter.13.cloned.1.call-start = ((), (), s32[]{:S(2)}) async-start(), calls=%async_computation.8 | async-start | bytes 10616832 | tf_op jit(solution)/shard_map/reduce_scatter | solution.py:83
  45.6 5.4 %collective-permute-start.7 = (f32[16,3,144]{2,0,1:T(8,128)S(1)}, f32[16,3,144]{2,0,1:T(8,128)S(1)}, u32[]{:S(2)}, u32[]{:S(2)}) collective-permute-start(f32[16,3,144]{2,0,1:T(8,128)S(1)} %fusion.72), channel_id=1, source_target_pairs={{0,1},{1,2},{2,3},{3,4},{4,5},{5,6},{6,7},{7,0},{8,9},{9,10},{10,1... | collective-permute-start | bytes 82952 | tf_op jit(solution)/shard_map/ppermute | solution.py:69
  51.0 6.5 %collective-permute-start.8 = (f32[16,3,144]{2,0,1:T(8,128)S(1)}, f32[16,3,144]{2,0,1:T(8,128)S(1)}, u32[]{:S(2)}, u32[]{:S(2)}) collective-permute-start(f32[16,3,144]{2,0,1:T(8,128)S(1)} %collective-permute-done.7), channel_id=1, source_target_pairs={{0,1},{1,2},{2,3},{3,4},{4,5},{5,6},{6,7},{7,0},{8,9},{9,10},{10,1... | collective-permute-start | bytes 82952 | tf_op jit(solution)/shard_map/ppermute | solution.py:69
  57.5 6.5 %collective-permute-start.9 = (f32[16,3,144]{2,0,1:T(8,128)S(1)}, f32[16,3,144]{2,0,1:T(8,128)S(1)}, u32[]{:S(2)}, u32[]{:S(2)}) collective-permute-start(f32[16,3,144]{2,0,1:T(8,128)S(1)} %collective-permute-done.8), channel_id=1, source_target_pairs={{0,1},{1,2},{2,3},{3,4},{4,5},{5,6},{6,7},{7,0},{8,9},{9,10},{10,1... | collective-permute-start | bytes 82952 | tf_op jit(solution)/shard_map/ppermute | solution.py:69
  64.0 6.5 %collective-permute-start.10 = (f32[16,3,144]{2,0,1:T(8,128)S(1)}, f32[16,3,144]{2,0,1:T(8,128)S(1)}, u32[]{:S(2)}, u32[]{:S(2)}) collective-permute-start(f32[16,3,144]{2,0,1:T(8,128)S(1)} %collective-permute-done.9), channel_id=1, source_target_pairs={{0,1},{1,2},{2,3},{3,4},{4,5},{5,6},{6,7},{7,0},{8,9},{9,10},{10,1... | collective-permute-start | bytes 82952 | tf_op jit(solution)/shard_map/ppermute | solution.py:69
  70.6 6.5 %collective-permute-start.11 = (f32[16,3,144]{2,0,1:T(8,128)S(1)}, f32[16,3,144]{2,0,1:T(8,128)S(1)}, u32[]{:S(2)}, u32[]{:S(2)}) collective-permute-start(f32[16,3,144]{2,0,1:T(8,128)S(1)} %collective-permute-done.10), channel_id=1, source_target_pairs={{0,1},{1,2},{2,3},{3,4},{4,5},{5,6},{6,7},{7,0},{8,9},{9,10},{10,1... | collective-permute-start | bytes 82952 | tf_op jit(solution)/shard_map/ppermute | solution.py:69
  77.1 6.5 %collective-permute-start.12 = (f32[16,3,144]{2,0,1:T(8,128)S(1)}, f32[16,3,144]{2,0,1:T(8,128)S(1)}, u32[]{:S(2)}, u32[]{:S(2)}) collective-permute-start(f32[16,3,144]{2,0,1:T(8,128)S(1)} %collective-permute-done.11), channel_id=1, source_target_pairs={{0,1},{1,2},{2,3},{3,4},{4,5},{5,6},{6,7},{7,0},{8,9},{9,10},{10,1... | collective-permute-start | bytes 82952 | tf_op jit(solution)/shard_map/ppermute | solution.py:69
  83.5 6.5 %collective-permute-start.13 = (f32[16,3,144]{2,0,1:T(8,128)S(1)}, f32[16,3,144]{2,0,1:T(8,128)S(1)}, u32[]{:S(2)}, u32[]{:S(2)}) collective-permute-start(f32[16,3,144]{2,0,1:T(8,128)S(1)} %collective-permute-done.12), channel_id=1, source_target_pairs={{0,1},{1,2},{2,3},{3,4},{4,5},{5,6},{6,7},{7,0},{8,9},{9,10},{10,1... | collective-permute-start | bytes 82952 | tf_op jit(solution)/shard_map/ppermute | solution.py:69
  121.6 155.3 %reduce-scatter.11.cloned.1.call-start = ((), (), s32[]{:S(2)}) async-start(), calls=%async_computation.7 | async-start | bytes 5308416 | tf_op jit(solution)/shard_map/reduce_scatter | solution.py:83
  123.3 5.0 collective-permute-start
  128.3 5.7 %collective-permute-start.1 = (f32[8,3,144]{2,0,1:T(8,128)S(1)}, f32[8,3,144]{2,0,1:T(8,128)S(1)}, u32[]{:S(2)}, u32[]{:S(2)}) collective-permute-start(f32[8,3,144]{2,0,1:T(8,128)S(1)} %collective-permute-done), channel_id=1, source_target_pairs={{0,1},{1,2},{2,3},{3,4},{4,5},{5,6},{6,7},{7,0},{8,9},{9,10},{10,1... | collective-permute-start | bytes 41480 | tf_op jit(solution)/shard_map/ppermute | solution.py:69
  134.0 5.7 %collective-permute-start.2 = (f32[8,3,144]{2,0,1:T(8,128)S(1)}, f32[8,3,144]{2,0,1:T(8,128)S(1)}, u32[]{:S(2)}, u32[]{:S(2)}) collective-permute-start(f32[8,3,144]{2,0,1:T(8,128)S(1)} %collective-permute-done.1), channel_id=1, source_target_pairs={{0,1},{1,2},{2,3},{3,4},{4,5},{5,6},{6,7},{7,0},{8,9},{9,10},{10,1... | collective-permute-start | bytes 41480 | tf_op jit(solution)/shard_map/ppermute | solution.py:69
  139.7 5.7 %collective-permute-start.3 = (f32[8,3,144]{2,0,1:T(8,128)S(1)}, f32[8,3,144]{2,0,1:T(8,128)S(1)}, u32[]{:S(2)}, u32[]{:S(2)}) collective-permute-start(f32[8,3,144]{2,0,1:T(8,128)S(1)} %collective-permute-done.2), channel_id=1, source_target_pairs={{0,1},{1,2},{2,3},{3,4},{4,5},{5,6},{6,7},{7,0},{8,9},{9,10},{10,1... | collective-permute-start | bytes 41480 | tf_op jit(solution)/shard_map/ppermute | solution.py:69
  145.4 5.7 %collective-permute-start.4 = (f32[8,3,144]{2,0,1:T(8,128)S(1)}, f32[8,3,144]{2,0,1:T(8,128)S(1)}, u32[]{:S(2)}, u32[]{:S(2)}) collective-permute-start(f32[8,3,144]{2,0,1:T(8,128)S(1)} %collective-permute-done.3), channel_id=1, source_target_pairs={{0,1},{1,2},{2,3},{3,4},{4,5},{5,6},{6,7},{7,0},{8,9},{9,10},{10,1... | collective-permute-start | bytes 41480 | tf_op jit(solution)/shard_map/ppermute | solution.py:69
  151.1 5.7 %collective-permute-start.5 = (f32[8,3,144]{2,0,1:T(8,128)S(1)}, f32[8,3,144]{2,0,1:T(8,128)S(1)}, u32[]{:S(2)}, u32[]{:S(2)}) collective-permute-start(f32[8,3,144]{2,0,1:T(8,128)S(1)} %collective-permute-done.4), channel_id=1, source_target_pairs={{0,1},{1,2},{2,3},{3,4},{4,5},{5,6},{6,7},{7,0},{8,9},{9,10},{10,1... | collective-permute-start | bytes 41480 | tf_op jit(solution)/shard_map/ppermute | solution.py:69
  156.8 5.7 %collective-permute-start.6 = (f32[8,3,144]{2,0,1:T(8,128)S(1)}, f32[8,3,144]{2,0,1:T(8,128)S(1)}, u32[]{:S(2)}, u32[]{:S(2)}) collective-permute-start(f32[8,3,144]{2,0,1:T(8,128)S(1)} %collective-permute-done.5), channel_id=1, source_target_pairs={{0,1},{1,2},{2,3},{3,4},{4,5},{5,6},{6,7},{7,0},{8,9},{9,10},{10,1... | collective-permute-start | bytes 41480 | tf_op jit(solution)/shard_map/ppermute | solution.py:69
  178.3 98.7 %copy-start.2 = (bf16[8,256,144]{1,2,0:T(8,128)(2,1)S(1)}, bf16[8,256,144]{1,2,0:T(8,128)(2,1)}, u32[]{:S(2)}) copy-start(bf16[8,256,144]{1,2,0:T(8,128)(2,1)} %param.14) | copy-start | bytes 1769476
  178.4 152.2 %all-gather.5.cloned.1.call-start = ((), (), s32[]{:S(2)}) async-start(), calls=%async_computation.9 | async-start | bytes 5308416 | tf_op jit(solution)/shard_map/all_gather | solution.py:146
  280.7 135.0 %reduce-scatter.17.cloned.1.call-start = ((), (), s32[]{:S(2)}) async-start(), calls=%async_computation.11 | async-start | bytes 5308416 | tf_op jit(solution)/shard_map/reduce_scatter | solution.py:160
  362.0 81.0 %reduce-scatter.19.cloned.1.call-start = ((), (), s32[]{:S(2)}) async-start(), calls=%async_computation.12 | async-start | bytes 737280
  367.1 107.5 %reduce-scatter.15.cloned.1.call-start = ((), (), s32[]{:S(2)}) async-start(), calls=%async_computation.10 | async-start | bytes 1474560 | tf_op jit(solution)/shard_map/reduce_scatter | solution.py:173
  373.5 132.7 %reduce-scatter.21.cloned.1.call-start = ((), (), s32[]{:S(2)}) async-start(), calls=%async_computation.13 | async-start | bytes 1474560
  421.7 87.7 %copy-start.1 = (bf16[1000,1152]{1,0:T(8,128)(2,1)S(1)}, bf16[1000,1152]{1,0:T(8,128)(2,1)}, u32[]{:S(2)}) copy-start(bf16[1000,1152]{1,0:T(8,128)(2,1)} %param.19) | copy-start | bytes 6912004
  (16 other events, 222.2 us)
Sparse Core Ops, SparseCore 0:
  41.1 52.6 all-gather.2
  121.8 99.7 reduce-scatter.12
  223.9 53.0 reduce-scatter.10
  280.9 49.6 all-gather.4
  362.1 53.6 reduce-scatter.16
  419.1 23.8 reduce-scatter.18
  445.9 28.6 reduce-scatter.14
  477.5 28.6 reduce-scatter.20
